TPU v7x, 32 devices: a whole 2x2x4 slice. The times are simulated.
32 devices in a mesh: dp: 2 (over x), mp: 16 (over z, y, core).
Axes of the slice: x: 2, y: 2, z: 4, core: 2. Of those that a mesh axis runs over, the one named last changes fastest.
Arguments:
- base_rows: bfloat16 [256, 8192], P('dp', 'mp'), may hold values from -6 to 6
- layer_rows: bfloat16 [256, 8192], P('dp', 'mp'), may hold values from -6 to 6
- cross_weight: bfloat16 [8192, 8192], P(None, 'mp'), may hold values from -0.0625 to 0.0625
- cross_bias: float32 [8192], P('mp'), may hold values from -3 to 3
- upstream: bfloat16 [256, 8192], P('dp', 'mp'), may hold values from -6 to 6
Outputs:
- crossed: bfloat16 [256, 8192], P('dp', 'mp')
- grad_base: bfloat16 [256, 8192], P('dp', 'mp')
- grad_layer: bfloat16 [256, 8192], P('dp', 'mp')
- grad_weight: float32 [8192, 8192], P('dp', 'mp')
- grad_bias: float32 [8192], P('mp')
All inputs are finite; a program needn't handle non-finite values.
Results may differ from a plain program's by a relative error of at most 0.0041.
Values may be sent and summed in bfloat16 or wider, within the bound.
No kernel may reach another device: no remote copies, remote signals or barrier semaphores. Data moves between devices by JAX's collectives and lax.ppermute only.
A program may use at most 128 MiB of HBM per device.

v0:
```python
import jax
import jax.numpy as jnp
from jax import lax
from jax.sharding import PartitionSpec as P


def local(base_rows, layer_rows, cross_weight, cross_bias, upstream):
    groups = lax.axis_size("dp")
    row_block = lax.all_to_all(cross_weight, "mp", split_axis=0, concat_axis=1, tiled=True)
    full_rows = lax.all_gather(layer_rows, "mp", axis=1, tiled=True)
    mixed = jnp.dot(full_rows, cross_weight, preferred_element_type=jnp.float32) + cross_bias
    base = base_rows.astype(jnp.float32)
    crossed = (base * mixed + layer_rows.astype(jnp.float32)).astype(jnp.bfloat16)
    upper = upstream.astype(jnp.float32)
    delta = upper * base
    delta_low = delta.astype(jnp.bfloat16)
    grad_base = (upper * mixed).astype(jnp.bfloat16)
    back = lax.dot_general(
        lax.all_gather(delta_low, "mp", axis=1, tiled=True),
        row_block,
        (((1,), (1,)), ((), ())),
        preferred_element_type=jnp.float32,
    )
    grad_layer = (upper + back).astype(jnp.bfloat16)
    scale = jnp.float32(base_rows.shape[0] * groups) ** (-0.5)
    grad_weight = (
        lax.psum_scatter(
            lax.dot_general(
                full_rows, delta_low, (((0,), (0,)), ((), ())), preferred_element_type=jnp.float32
            ),
            "dp",
            scatter_dimension=0,
            tiled=True,
        )
        * scale
    )
    grad_bias = lax.psum(jnp.sum(delta, axis=0), "dp") * scale
    return (crossed, grad_base, grad_layer, grad_weight, grad_bias)


def solution(mesh):
    return jax.shard_map(
        local,
        mesh=mesh,
        in_specs=(P("dp", "mp"), P("dp", "mp"), P(None, "mp"), P("mp"), P("dp", "mp")),
        out_specs=(P("dp", "mp"), P("dp", "mp"), P("dp", "mp"), P("dp", "mp"), P("mp")),
        check_vma=False,
    )
```

profile of v0, /device:TPU:0, one launch (start us, length us, event | category | flops | bytes accessed | tf_op | source)
XLA Modules:
  0.0 428.7 jit_solution(16000133492980373238)
XLA Ops:
  7.2 0.0 all-gather.3.cloned.1.call-start
  7.2 0.7 all-gather.3.cloned.1.call-update
  7.9 0.0 all-gather.5.cloned.1.call-start
  7.9 46.0 %all-gather.3.cloned.1.call-done = bf16[128,8192]{1,0:T(8,128)(2,1)} async-done(((bf16[128,512]{1,0:T(8,128)(2,1)}), bf16[128,8192]{1,0:T(8,128)(2,1)}) %all-gather.3.cloned.1.call-update) | async-done | bytes 2097168 | tf_op jit(solution)/shard_map/all_gather | solution.py:10
  53.9 0.0 copy-start
  53.9 6.2 %fusion.3 = (bf16[128,512]{1,0:T(8,128)(2,1)}, bf16[128,512]{1,0:T(8,128)(2,1)}, bf16[128,512]{1,0:T(8,128)(2,1)}, f32[512]{0:T(512)S(1)}) fusion(bf16[128,512]{1,0:T(8,128)(2,1)} %param.9, bf16[128,512]{1,0:T(8,128)(2,1)} %param.6, bf16[128,512]{1,0:T(8,128)(2,1)} %param.5, f32[512]{0:T(512)} %param.8, bf16[128,8192]{1,0:T(8,128)(2,1)} %all-gather.3.cloned.1.call-done, ...), kind=kOutput, calls=%fused_computation.10 | convolution fusion | flops 1074527744 | bytes 11276288 | tf_op jit(solution)/shard_map/dot_general | solution.py:11
  60.1 0.0 all-gather.5.cloned.1.call-update
  60.2 0.0 reduce-scatter.2.cloned.1.call-start
  60.2 0.0 copy-done
  60.2 9.0 %convolution_bitcast_fusion = f32[8192,512]{0,1:T(8,128)} fusion(bf16[128,512]{1,0:T(8,128)(2,1)} %get-tuple-element.24, bf16[128,8192]{1,0:T(8,128)(2,1)S(1)} %copy-done), kind=kOutput, calls=%fused_computation | convolution fusion | flops 1073741824 | bytes 19005440 | tf_op jit(solution)/shard_map/dot_general | solution.py:28
  69.2 0.0 reduce-scatter.2.cloned.1.call-update
  69.2 4.8 %all-to-all-start = ((bf16[16,512,512]{2,1,0:T(8,128)(2,1)}), bf16[16,512,512]{2,1,0:T(8,128)(2,1)}, u32[]{:S(2)}, u32[]{:S(2)}) async-start(bf16[16,512,512]{2,1,0:T(8,128)(2,1)} %bitcast.12), calls=%async_computation | async-start | bytes 16777216 | tf_op jit(solution)/shard_map/all_to_all | solution.py:9
  74.0 4.9 %psum.7 = f32[512]{0:T(512)S(1)} all-reduce(f32[512]{0:T(512)S(1)} %get-tuple-element.25), channel_id=1, replica_groups=mesh['dp'=2,'mp'=16] {'dp'}, use_global_device_ids=true, to_apply=%region_2.0 | all-reduce | flops 512 | bytes 4096 | tf_op jit(solution)/shard_map/psum | solution.py:37
  79.0 0.6 broadcast_multiply_fusion.1
  79.6 154.0 %all-to-all-done = bf16[16,512,512]{2,1,0:T(8,128)(2,1)} async-done(((bf16[16,512,512]{2,1,0:T(8,128)(2,1)}), bf16[16,512,512]{2,1,0:T(8,128)(2,1)}, u32[]{:S(2)}, u32[]{:S(2)}) %all-to-all-start) | async-done | bytes 8388640 | tf_op jit(solution)/shard_map/all_to_all | solution.py:9
  233.6 0.0 copy-start.1
  233.6 12.3 %copy.12 = bf16[512,16,512]{0,2,1:T(8,128)(2,1)} copy(bf16[512,16,512]{2,0,1:T(8,128)(2,1)} %bitcast.1) | data formatting | bytes 16777216 | tf_op jit(solution)/shard_map/all_to_all | solution.py:9
  245.9 0.0 all-gather.5.cloned.1.call-done
  245.9 0.0 copy-done.1
  245.9 6.2 %fusion = bf16[128,512]{1,0:T(8,128)(2,1)} fusion(bf16[128,8192]{1,0:T(8,128)(2,1)} %all-gather.5.cloned.1.call-done, bf16[512,8192]{0,1:T(8,128)(2,1)} %bitcast.11, bf16[128,512]{1,0:T(8,128)(2,1)S(1)} %copy-done.1), kind=kOutput, calls=%fused_computation.4 | convolution fusion | flops 1073938432 | bytes 10747904 | tf_op jit(solution)/shard_map/dot_general | solution.py:18
  252.1 153.4 %reduce-scatter.2.cloned.1.call-done = f32[4096,512]{0,1:T(8,128)} async-done(((f32[8192,512]{0,1:T(8,128)}), f32[4096,512]{0,1:T(8,128)}) %reduce-scatter.2.cloned.1.call-update) | async-done | bytes 8388624 | tf_op jit(solution)/shard_map/reduce_scatter | solution.py:27
  405.5 7.8 %broadcast_multiply_fusion = f32[4096,512]{0,1:T(8,128)} fusion(f32[4096,512]{0,1:T(8,128)} %reduce-scatter.2.cloned.1.call-done), kind=kLoop, calls=%fused_computation.1 | loop fusion | flops 2097152 | bytes 16777216 | tf_op jit(solution)/shard_map/mul | solution.py:27
  413.3 8.9 %copy.13 = f32[4096,512]{1,0:T(8,128)} copy(f32[4096,512]{0,1:T(8,128)} %broadcast_multiply_fusion) | data formatting | bytes 16777216
Async XLA Ops:
  7.2 46.8 %all-gather.3.cloned.1.call-start = ((), (), s32[]{:S(2)}) async-start(), calls=%async_computation.2 | async-start | bytes 2228224 | tf_op jit(solution)/shard_map/all_gather | solution.py:10
  7.9 238.0 %all-gather.5.cloned.1.call-start = ((), (), s32[]{:S(2)}) async-start(), calls=%async_computation.3 | async-start | bytes 2228224 | tf_op jit(solution)/shard_map/all_gather | solution.py:19
  53.9 6.3 %copy-start = (bf16[128,8192]{1,0:T(8,128)(2,1)S(1)}, bf16[128,8192]{1,0:T(8,128)(2,1)}, u32[]{:S(2)}) copy-start(bf16[128,8192]{1,0:T(8,128)(2,1)} %all-gather.3.cloned.1.call-done) | copy-start | bytes 6291460
  60.2 345.3 %reduce-scatter.2.cloned.1.call-start = ((), (), s32[]{:S(2)}) async-start(), calls=%async_computation.4 | async-start | bytes 25165824 | tf_op jit(solution)/shard_map/reduce_scatter | solution.py:27
  69.2 164.3 %all-to-all-start = ((bf16[16,512,512]{2,1,0:T(8,128)(2,1)}), bf16[16,512,512]{2,1,0:T(8,128)(2,1)}, u32[]{:S(2)}, u32[]{:S(2)}) async-start(bf16[16,512,512]{2,1,0:T(8,128)(2,1)} %bitcast.12), calls=%async_computation | async-start | bytes 16777216 | tf_op jit(solution)/shard_map/all_to_all | solution.py:9
  233.6 12.3 %copy-start.1 = (bf16[128,512]{1,0:T(8,128)(2,1)S(1)}, bf16[128,512]{1,0:T(8,128)(2,1)}, u32[]{:S(2)}) copy-start(bf16[128,512]{1,0:T(8,128)(2,1)} %param.9) | copy-start | bytes 393220
Sparse Core Ops, SparseCore 0:
  10.1 43.7 all-gather.2
  60.3 143.4 all-gather.4
  206.1 199.3 reduce-scatter.1
where the time goes:
time: 429 us
  waiting for transfers between devices  354 us (83%)
  matrix products  21.4 us (5%)
  local copies, waits for them, and re-layouts  21.3 us (5%)
  between operations  13.8 us (3%)
  other arithmetic  8.35 us (2%)
  blocking collectives  4.93 us (1%)
  starting transfers between devices  4.92 us (1%)
    all_to_all x1, waiting for transfers between devices, local(): lax.all_to_all(cross_weight, 'mp', split_axis=0, concat_axis=1, tiled=True)  154 us
    reduce_scatter x1, waiting for transfers between devices, local(): lax.psum_scatter(lax.dot_general(full_rows, delta_low, (((0,), (0,)), (()...  153 us
    all_gather x1, waiting for transfers between devices, local(): full_rows = lax.all_gather(layer_rows, 'mp', axis=1, tiled=True)  46 us
    all_to_all x1, local copies, waits for them, and re-layouts, local(): lax.all_to_all(cross_weight, 'mp', split_axis=0, concat_axis=1, tiled=True)  12.3 us
    dot_general x1, matrix products, local(): lax.dot_general(full_rows, delta_low, (((0,), (0,)), ((), ())), preferred...  8.99 us
    unnamed x5, local copies, waits for them, and re-layouts  8.95 us
  transfers between devices with their start and end apart: 4, of which 3 were waited for; matrix products, arithmetic and copies ran while one was open for 7% of the time, Pallas kernels for 0%

commit v1 on v0

--- a/solution.py
+++ b/solution.py
@@ -6,7 +6,10 @@
 
 def local(base_rows, layer_rows, cross_weight, cross_bias, upstream):
     groups = lax.axis_size("dp")
-    row_block = lax.all_to_all(cross_weight, "mp", split_axis=0, concat_axis=1, tiled=True)
+    row_block = jnp.concatenate(
+        lax.all_to_all(jnp.stack(jnp.split(cross_weight, lax.axis_size("mp"), axis=0)), "mp", 0, 0),
+        axis=1,
+    )
     full_rows = lax.all_gather(layer_rows, "mp", axis=1, tiled=True)
     mixed = jnp.dot(full_rows, cross_weight, preferred_element_type=jnp.float32) + cross_bias
     base = base_rows.astype(jnp.float32)

time: 429 us -> 336 us (0.78)
  the two profiles are of different devices: /device:TPU:0 before, /device:TPU:15 now
where the time goes in v1:
time: 336 us; the launch traced here: 335 us
  waiting for transfers between devices  223 us (66%)
  local copies, waits for them, and re-layouts  59.1 us (18%)
  matrix products  21.2 us (6%)
  between operations  13.8 us (4%)
  other arithmetic  8.35 us (2%)
  starting transfers between devices  5.69 us (2%)
  blocking collectives  4.38 us (1%)
    all_to_all x1, waiting for transfers between devices, local(): lax.all_to_all(jnp.stack(jnp.split(cross_weight, lax.axis_size('mp'), axi...  177 us
    unnamed x42, local copies, waits for them, and re-layouts  52.5 us
    all_gather x1, waiting for transfers between devices, local(): full_rows = lax.all_gather(layer_rows, 'mp', axis=1, tiled=True)  44.5 us
    dot_general x1, matrix products, local(): lax.dot_general(full_rows, delta_low, (((0,), (0,)), ((), ())), preferred...  9 us
    mul x1, other arithmetic, local(): lax.psum_scatter(lax.dot_general(full_rows, delta_low, (((0,), (0,)), (()...  7.76 us
  transfers between devices with their start and end apart: 4, of which 2 were waited for; matrix products, arithmetic and copies ran while one was open for 20% of the time, Pallas kernels for 0%

profile of v1, /device:TPU:15, one launch (start us, length us, event | category | flops | bytes accessed | tf_op | source)
XLA Modules:
  0.0 335.1 jit_solution(14075404648504498726)
XLA Ops:
  7.2 0.0 all-gather.3.cloned.1.call-start
  7.2 0.7 all-gather.3.cloned.1.call-update
  7.9 0.0 all-gather.5.cloned.1.call-start
  7.9 44.5 %all-gather.3.cloned.1.call-done = bf16[128,8192]{1,0:T(8,128)(2,1)} async-done(((bf16[128,512]{1,0:T(8,128)(2,1)}), bf16[128,8192]{1,0:T(8,128)(2,1)}) %all-gather.3.cloned.1.call-update) | async-done | bytes 2097168 | tf_op jit(solution)/shard_map/all_gather | solution.py:13
  52.4 0.0 copy-start
  52.4 6.2 %fusion.3 = (bf16[128,512]{1,0:T(8,128)(2,1)}, bf16[128,512]{1,0:T(8,128)(2,1)}, bf16[128,512]{1,0:T(8,128)(2,1)}, f32[512]{0:T(512)S(1)}) fusion(bf16[128,512]{1,0:T(8,128)(2,1)} %param.9, bf16[128,512]{1,0:T(8,128)(2,1)} %param.6, bf16[128,512]{1,0:T(8,128)(2,1)} %param.5, f32[512]{0:T(512)} %param.8, bf16[128,8192]{1,0:T(8,128)(2,1)} %all-gather.3.cloned.1.call-done, ...), kind=kOutput, calls=%fused_computation.26 | convolution fusion | flops 1074527744 | bytes 11276288 | tf_op jit(solution)/shard_map/dot_general | solution.py:14
  58.7 0.0 all-gather.5.cloned.1.call-update
  58.7 0.0 reduce-scatter.2.cloned.1.call-start
  58.7 0.0 copy-done
  58.7 9.0 %convolution_bitcast_fusion = f32[8192,512]{0,1:T(8,128)} fusion(bf16[128,512]{1,0:T(8,128)(2,1)} %get-tuple-element.35, bf16[128,8192]{1,0:T(8,128)(2,1)S(1)} %copy-done), kind=kOutput, calls=%fused_computation | convolution fusion | flops 1073741824 | bytes 19005440 | tf_op jit(solution)/shard_map/dot_general | solution.py:31
  67.7 0.0 reduce-scatter.2.cloned.1.call-update
  67.8 5.7 %fusion.6 = (bf16[512,512]{1,0:T(8,128)(2,1)S(1)}, bf16[512,512]{1,0:T(8,128)(2,1)S(1)}, bf16[512,512]{1,0:T(8,128)(2,1)S(1)}, bf16[512,512]{1,0:T(8,128)(2,1)S(...) fusion(bf16[8192,512]{1,0:T(8,128)(2,1)} %param.7), kind=kLoop, calls=%fused_computation.30 | loop fusion | bytes 16777216 | tf_op jit(solution)/shard_map/split | solution.py:10
  73.5 2.1 copy.28
  75.6 2.1 copy.29
  77.7 2.0 copy.30
  79.7 2.0 copy.31
  81.8 2.1 copy.32
  83.8 2.1 copy.33
  85.9 2.1 copy.34
  88.0 2.0 copy.35
  90.0 2.1 copy.36
  92.1 2.1 copy.37
  94.1 1.0 copy.38
  95.1 0.2 copy.39
  95.3 0.2 copy.40
  95.6 0.2 copy.41
  95.8 0.2 copy.42
  96.0 0.2 copy.43
  96.2 0.0 copy-start.3
  96.2 0.0 copy-start.2
  96.2 0.0 copy-start.1
  96.2 2.0 bitcast_dynamic-update-slice_fusion.15
  98.2 1.9 bitcast_dynamic-update-slice_fusion.14
  100.1 1.9 bitcast_dynamic-update-slice_fusion.13
  102.0 1.9 bitcast_dynamic-update-slice_fusion.12
  103.8 1.9 bitcast_dynamic-update-slice_fusion.11
  105.7 1.9 bitcast_dynamic-update-slice_fusion.10
  107.6 1.9 bitcast_dynamic-update-slice_fusion.9
  109.5 1.9 bitcast_dynamic-update-slice_fusion.8
  111.3 0.0 copy-done.3
  111.3 0.8 bitcast_dynamic-update-slice_fusion.7
  112.2 0.0 copy-done.2
  112.2 0.8 bitcast_dynamic-update-slice_fusion.6
  113.0 0.0 copy-done.1
  113.0 0.8 bitcast_dynamic-update-slice_fusion.5
  113.8 0.8 bitcast_dynamic-update-slice_fusion.4
  114.7 0.8 bitcast_dynamic-update-slice_fusion.3
  115.5 0.8 bitcast_dynamic-update-slice_fusion.2
  116.3 0.8 bitcast_dynamic-update-slice_fusion.1
  117.1 0.8 bitcast_dynamic-update-slice_fusion
  118.0 0.0 copy-start.4
  118.0 5.6 %all-to-all-start = ((bf16[16,512,512]{1,2,0:T(8,128)(2,1)}), bf16[16,512,512]{1,2,0:T(8,128)(2,1)}, u32[]{:S(2)}, u32[]{:S(2)}) async-start(bf16[16,512,512]{1,2,0:T(8,128)(2,1)} %bitcast_dynamic-update-slice_fusion), calls=%async_computation | async-start | bytes 16777216 | tf_op jit(solution)/shard_map/all_to_all | solution.py:10
  123.5 4.4 %psum.7 = f32[512]{0:T(512)S(1)} all-reduce(f32[512]{0:T(512)S(1)} %get-tuple-element.36), channel_id=1, replica_groups=mesh['dp'=2,'mp'=16] {'dp'}, use_global_device_ids=true, to_apply=%region_2.0 | all-reduce | flops 512 | bytes 4096 | tf_op jit(solution)/shard_map/psum | solution.py:40
  127.9 0.6 broadcast_multiply_fusion.1
  128.5 0.0 all-gather.5.cloned.1.call-done
  128.5 177.4 %all-to-all-done = bf16[16,512,512]{1,2,0:T(8,128)(2,1)} async-done(((bf16[16,512,512]{1,2,0:T(8,128)(2,1)}), bf16[16,512,512]{1,2,0:T(8,128)(2,1)}, u32[]{:S(2)}, u32[]{:S(2)}) %all-to-all-start) | async-done | bytes 8388640 | tf_op jit(solution)/shard_map/all_to_all | solution.py:10
  305.9 0.0 copy-done.4
  305.9 5.9 %fusion = bf16[128,512]{1,0:T(8,128)(2,1)} fusion(bf16[128,8192]{1,0:T(8,128)(2,1)} %all-gather.5.cloned.1.call-done, bf16[512,8192]{0,1:T(8,128)(2,1)} %bitcast.17, bf16[128,512]{1,0:T(8,128)(2,1)S(1)} %copy-done.4), kind=kOutput, calls=%fused_computation.4 | convolution fusion | flops 1073938432 | bytes 10747904 | tf_op jit(solution)/shard_map/dot_general | solution.py:21
  311.8 0.0 reduce-scatter.2.cloned.1.call-done
  311.9 7.8 %broadcast_multiply_fusion = f32[4096,512]{0,1:T(8,128)} fusion(f32[4096,512]{0,1:T(8,128)} %reduce-scatter.2.cloned.1.call-done), kind=kLoop, calls=%fused_computation.1 | loop fusion | flops 2097152 | bytes 16777216 | tf_op jit(solution)/shard_map/mul | solution.py:30
  319.6 8.9 %copy.27 = f32[4096,512]{1,0:T(8,128)} copy(f32[4096,512]{0,1:T(8,128)} %broadcast_multiply_fusion) | data formatting | bytes 16777216
Async XLA Ops:
  7.2 45.3 %all-gather.3.cloned.1.call-start = ((), (), s32[]{:S(2)}) async-start(), calls=%async_computation.2 | async-start | bytes 2228224 | tf_op jit(solution)/shard_map/all_gather | solution.py:13
  7.9 120.6 %all-gather.5.cloned.1.call-start = ((), (), s32[]{:S(2)}) async-start(), calls=%async_computation.3 | async-start | bytes 2228224 | tf_op jit(solution)/shard_map/all_gather | solution.py:22
  52.4 6.3 %copy-start = (bf16[128,8192]{1,0:T(8,128)(2,1)S(1)}, bf16[128,8192]{1,0:T(8,128)(2,1)}, u32[]{:S(2)}) copy-start(bf16[128,8192]{1,0:T(8,128)(2,1)} %all-gather.3.cloned.1.call-done) | copy-start | bytes 6291460
  58.7 253.2 %reduce-scatter.2.cloned.1.call-start = ((), (), s32[]{:S(2)}) async-start(), calls=%async_computation.4 | async-start | bytes 25165824 | tf_op jit(solution)/shard_map/reduce_scatter | solution.py:30
  96.2 15.1 %copy-start.3 = (bf16[512,512]{0,1:T(8,128)(2,1)S(1)}, bf16[512,512]{0,1:T(8,128)(2,1)}, u32[]{:S(2)}) copy-start(bf16[512,512]{0,1:T(8,128)(2,1)} %copy.36) | copy-start | bytes 1572868
  96.2 15.9 %copy-start.2 = (bf16[512,512]{0,1:T(8,128)(2,1)S(1)}, bf16[512,512]{0,1:T(8,128)(2,1)}, u32[]{:S(2)}) copy-start(bf16[512,512]{0,1:T(8,128)(2,1)} %copy.37) | copy-start | bytes 1572868
  96.2 16.8 %copy-start.1 = (bf16[512,512]{0,1:T(8,128)(2,1)S(1)}, bf16[512,512]{0,1:T(8,128)(2,1)}, u32[]{:S(2)}) copy-start(bf16[512,512]{0,1:T(8,128)(2,1)} %copy.38) | copy-start | bytes 1572868
  118.0 187.9 %copy-start.4 = (bf16[128,512]{1,0:T(8,128)(2,1)S(1)}, bf16[128,512]{1,0:T(8,128)(2,1)}, u32[]{:S(2)}) copy-start(bf16[128,512]{1,0:T(8,128)(2,1)} %param.9) | copy-start | bytes 393220
  118.0 187.9 %all-to-all-start = ((bf16[16,512,512]{1,2,0:T(8,128)(2,1)}), bf16[16,512,512]{1,2,0:T(8,128)(2,1)}, u32[]{:S(2)}, u32[]{:S(2)}) async-start(bf16[16,512,512]{1,2,0:T(8,128)(2,1)} %bitcast_dynamic-update-slice_fusion), calls=%async_computation | async-start | bytes 16777216 | tf_op jit(solution)/shard_map/all_to_all | solution.py:10
Sparse Core Ops, SparseCore 0:
  10.1 42.2 all-gather.2
  58.8 40.1 all-gather.4
  101.3 187.1 reduce-scatter.1
